TPU v7x, 32 devices: a whole 2x2x4 slice. The times are simulated.
32 devices in a mesh: ta: 4 (over z), gz: 4 (over x, core), xy: 2 (over y).
Axes of the slice: x: 2, y: 2, z: 4, core: 2. Of those that a mesh axis runs over, the one named last changes fastest.
Arguments:
- links: float32 [4, 2, 3, 3, 4, 8, 512], P(None, None, None, None, 'ta', 'xy', 'gz'), may hold values from -0.72 to 1.72
- guess: float32 [12, 2, 4, 3, 4, 8, 512], P(None, None, None, None, 'ta', 'xy', 'gz'), may hold values from -1.5 to 1.5
- source_sites: int32 [4, 2, 4, 4], P('ta', 'xy', 'gz'), may hold values from 0 to 31, as said below
Outputs:
- solution: float32 [12, 2, 4, 3, 4, 8, 512], P(None, None, None, None, 'ta', 'xy', 'gz')
- residual: float32 [12, 2, 4, 3, 4, 8, 512], P(None, None, None, None, 'ta', 'xy', 'gz')
Inputs may be any that keep to these rules, and one draw needn't show every extreme that they name: `source_sites`: each entry is an offset inside its block: time below 1, y below 4, z below 4, x below 32.
All inputs are finite; a program needn't handle non-finite values.
Results may differ from a plain program's by a relative error of at most 0.00012.
Values sent between devices are 32-bit elements; how exact they have to be, the bound alone decides.
A program may use at most 128 MiB of HBM per device.

v0:
```python
import functools

import jax
import jax.numpy as jnp
from jax import lax
from jax.experimental import pallas as pl
from jax.experimental.pallas import tpu as pltpu
from jax.sharding import PartitionSpec as P

LX = 32
NSMEAR = 8
HOP = 0.12
PAIRS = 6
MESH = pl.DeviceIdType.MESH
AXES = ("xy", "gz", "ta")

E_ROWS = (
    ((1, -1j), (0, -1j)),
    ((1, -1), (0, 1)),
    ((0, -1j), (1, 1j)),
    ((0, 1), (1, 1)),
)


def times(coef, z):
    re, im = z
    if coef == 1:
        return (1, re), (1, im)
    if coef == -1:
        return (-1, re), (-1, im)
    if coef == 1j:
        return (-1, im), (1, re)
    return (1, im), (-1, re)


def add_term(z, coef, other):
    out = []
    for base, (sign, term) in zip(z, times(coef, other)):
        out.append(base + term if sign > 0 else base - term)
    return tuple(out)


def project(f, mu, parity):
    half = []
    for row in range(2):
        column, coef = E_ROWS[mu][row]
        half.append([add_term(f[row][a], parity * coef, f[2 + column][a]) for a in range(3)])
    return half


def lift_add(total, h, mu, parity):
    for row in range(2):
        column, coef = E_ROWS[mu][row]
        for a in range(3):
            total[row][a] = add_term(total[row][a], 1, h[row][a])
            low = parity * complex(coef).conjugate()
            total[2 + column][a] = add_term(total[2 + column][a], low, h[row][a])


def link_times(link, mu, vectors, adjoint):
    def entry(a, b):
        if adjoint:
            a, b = b, a
        base = mu * 18 + a * 3 + b
        return link[base], link[base + 9]

    out = [[None] * 3 for _ in vectors]
    for a in range(3):
        totals = [None] * len(vectors)
        for b in range(3):
            ur, ui = entry(a, b)
            for k, vec in enumerate(vectors):
                re, im = vec[b]
                if adjoint:
                    tr, ti = ur * re + ui * im, ur * im - ui * re
                else:
                    tr, ti = ur * re - ui * im, ur * im + ui * re
                old = totals[k]
                totals[k] = (tr, ti) if old is None else (old[0] + tr, old[1] + ti)
        for k in range(len(vectors)):
            out[k][a] = totals[k]
    return out


def flat(vectors):
    return [vec[a][part] for part in range(2) for vec in vectors for a in range(3)]


def unflat(items, count):
    return [
        [(items[k * 3 + a], items[3 * count + k * 3 + a]) for a in range(3)] for k in range(count)
    ]


class Shifts:
    def __init__(self):
        row = lax.broadcasted_iota(jnp.int32, (8, 128), 0)
        lane = lax.broadcasted_iota(jnp.int32, (8, 128), 1)
        self.low = row < 4
        self.lane = lane
        self.place = ([row % 4 == k for k in range(4)], [lane // LX == k for k in range(4)])
        self.x_first = lane % LX == 0
        self.x_last = lane % LX == LX - 1
        self.unit = ((0, 1, 8), (1, LX, 128))

    def roll(self, v, kind, steps):
        axis, unit, size = self.unit[kind]
        amount = (steps * unit) % size
        return v if amount == 0 else pltpu.roll(v, amount, axis)

    def pack(self, items, kind, ahead):
        packed = []
        for g in range(0, len(items), 4):
            out = None
            for k in range(4):
                v = self.roll(items[g + k], kind, k if ahead else k - 3)
                out = v if out is None else jnp.where(self.place[kind][k], v, out)
            packed.append(out)
        return packed

    def shift(self, items, packed, kind, ahead):
        outs = []
        for i, v in enumerate(items):
            got = packed[i // 4]
            k = i % 4
            if ahead:
                moved = self.roll(v, kind, -1)
                outs.append(jnp.where(self.place[kind][3], self.roll(got, kind, 3 - k), moved))
            else:
                moved = self.roll(v, kind, 1)
                outs.append(jnp.where(self.place[kind][0], self.roll(got, kind, -k), moved))
        return outs

    def along_x(self, items, ahead):
        outs = []
        for v in items:
            if ahead:
                a, b = pltpu.roll(v, 127, 1), pltpu.roll(v, LX - 1, 1)
                outs.append(jnp.where(self.x_last, b, a))
            else:
                a, b = pltpu.roll(v, 1, 1), pltpu.roll(v, 129 - LX, 1)
                outs.append(jnp.where(self.x_first, b, a))
        return outs


def kernel(
    sizes, sites_ref, links_ref, guess_ref, sol_ref, res_ref,
    link, guess, field_a, field_b, search, acc, right, carried,
    edge_out, edge_in, time_out, time_in, sm_out, sm_in, smt_out, smt_in,
    red_out, red_in, sums,
    edge_sem, time_sem, w_send, sm_sem, smt_sem, s_send, red_sem, r_send,
):
    n_of = dict(zip(AXES, sizes))
    me = {axis: lax.axis_index(axis) for axis in AXES}

    def peer(axis, step):
        return {axis: lax.rem(me[axis] + step + n_of[axis], n_of[axis])}

    barrier = pltpu.get_barrier_semaphore()
    for axis in AXES:
        for k in range(1, n_of[axis]):
            pl.semaphore_signal(barrier, inc=1, device_id=peer(axis, k), device_id_type=MESH)

    sh = Shifts()

    sign = jnp.where(me["ta"] == n_of["ta"] - 1, -1.0, 1.0).astype(jnp.float32)
    for i in range(72):
        v = links_ref[i]
        if i >= 54:
            v = v * sign
        link[i, 0:4, :] = v
        link[i, 4:8, :] = v

    def rhs_of(p):
        first = jnp.where(p < 4, 3 * p, 6 * p - 22)
        second = jnp.where(p < 4, 3 * p + 1, 6 * p - 19)
        return first, second

    def load_guess(p, _):
        first, second = rhs_of(p)
        for i in range(24):
            guess[p, i, 0:4, :] = guess_ref[first, i]
            guess[p, i, 4:8, :] = guess_ref[second, i]
        return _

    lax.fori_loop(0, PAIRS, load_guess, 0)
    pl.semaphore_wait(barrier, sum(n - 1 for n in sizes))

    def edge_copy(w, d, p):
        axis, step = (("xy", -1), ("xy", 1), ("gz", -1), ("gz", 1))[d]
        return pltpu.make_async_remote_copy(
            src_ref=edge_out.at[w, d, p], dst_ref=edge_in.at[w, d, p],
            send_sem=w_send.at[w, d, p], recv_sem=edge_sem.at[w, d, p],
            device_id=peer(axis, step), device_id_type=MESH,
        )

    def time_copy(w, d, p):
        return pltpu.make_async_remote_copy(
            src_ref=time_out.at[w, d, p], dst_ref=time_in.at[w, d, p],
            send_sem=w_send.at[w, 4 + d, p], recv_sem=time_sem.at[w, d, p],
            device_id=peer("ta", (-1, 1)[d]), device_id_type=MESH,
        )

    def load_field(ref, p):
        return unflat([ref[p, i] for i in range(24)], 4)

    def send_body(f, w, p, par):
        for i, v in enumerate(flat(project(f, 3, -par))):
            time_out[w, 0, p, i] = v
        time_copy(w, 0, p).start()
        for i, v in enumerate(flat(link_times(link, 3, project(f, 3, par), True))):
            time_out[w, 1, p, i] = v
        time_copy(w, 1, p).start()
        for kind, mu in ((0, 1), (1, 2)):
            for i, v in enumerate(sh.pack(flat(project(f, mu, -par)), kind, True)):
                edge_out[w, 2 * kind, p, i] = v
            edge_copy(w, 2 * kind, p).start()
            behind = flat(link_times(link, mu, project(f, mu, par), True))
            for i, v in enumerate(behind):
                carried[kind, p, i] = v
            for i, v in enumerate(sh.pack(behind, kind, False)):
                edge_out[w, 2 * kind + 1, p, i] = v
            edge_copy(w, 2 * kind + 1, p).start()

    def interior(src, par):
        def body(p, _):
            f = load_field(src, p)
            zero = jnp.zeros((8, 128), jnp.float32)
            total = [[(zero, zero)] * 3 for _ in range(4)]
            ahead = unflat(sh.along_x(flat(project(f, 0, -par)), True), 2)
            lift_add(total, link_times(link, 0, ahead, False), 0, -par)
            behind = flat(link_times(link, 0, project(f, 0, par), True))
            lift_add(total, unflat(sh.along_x(behind, False), 2), 0, par)
            for i, v in enumerate(flat(total)):
                acc[p, i] = v
            return _
        lax.fori_loop(0, PAIRS, body, 0)

    def receive_body(src, w, p, par):
        f = load_field(src, p)
        total = load_field(acc, p)
        for kind, mu in ((0, 1), (1, 2)):
            edge_copy(w, 2 * kind, p).wait_recv()
            got = [edge_in[w, 2 * kind, p, i] for i in range(3)]
            ahead = unflat(sh.shift(flat(project(f, mu, -par)), got, kind, True), 2)
            lift_add(total, link_times(link, mu, ahead, False), mu, -par)
            edge_copy(w, 2 * kind + 1, p).wait_recv()
            got = [edge_in[w, 2 * kind + 1, p, i] for i in range(3)]
            local = [carried[kind, p, i] for i in range(12)]
            lift_add(total, unflat(sh.shift(local, got, kind, False), 2), mu, par)
        time_copy(w, 0, p).wait_recv()
        ahead = unflat([time_in[w, 0, p, i] for i in range(12)], 2)
        lift_add(total, link_times(link, 3, ahead, False), 3, -par)
        time_copy(w, 1, p).wait_recv()
        lift_add(total, unflat([time_in[w, 1, p, i] for i in range(12)], 2), 3, par)
        return [a - HOP * b for a, b in zip(flat(f), flat(total))]

    def sm_copy(step, d):
        axis, hop = (("xy", -1), ("xy", 1), ("gz", -1), ("gz", 1))[d]
        return pltpu.make_async_remote_copy(
            src_ref=sm_out.at[step, d], dst_ref=sm_in.at[step, d],
            send_sem=s_send.at[step, d], recv_sem=sm_sem.at[step, d],
            device_id=peer(axis, hop), device_id_type=MESH,
        )

    def smt_copy(d):
        return pltpu.make_async_remote_copy(
            src_ref=smt_out.at[d], dst_ref=smt_in.at[d],
            send_sem=s_send.at[NSMEAR + 1, d], recv_sem=smt_sem.at[d],
            device_id=peer("ta", (-1, 1)[d]), device_id_type=MESH,
        )

    def colour_hops(items, step):
        vectors = unflat(items, 2)
        behinds = []
        for kind, mu in ((0, 1), (1, 2)):
            for i, v in enumerate(sh.pack(items, kind, True)):
                sm_out[step, 2 * kind, i] = v
            sm_copy(step, 2 * kind).start()
            behind = flat(link_times(link, mu, vectors, True))
            behinds.append(behind)
            for i, v in enumerate(sh.pack(behind, kind, False)):
                sm_out[step, 2 * kind + 1, i] = v
            sm_copy(step, 2 * kind + 1).start()
        aheads_out = [flat(link_times(link, 0, unflat(sh.along_x(items, True), 2), False))]
        behinds_out = [sh.along_x(flat(link_times(link, 0, vectors, True)), False)]
        for kind, mu in ((0, 1), (1, 2)):
            sm_copy(step, 2 * kind).wait_recv()
            got = [sm_in[step, 2 * kind, i] for i in range(3)]
            ahead = unflat(sh.shift(items, got, kind, True), 2)
            aheads_out.append(flat(link_times(link, mu, ahead, False)))
            sm_copy(step, 2 * kind + 1).wait_recv()
            got = [sm_in[step, 2 * kind + 1, i] for i in range(3)]
            behinds_out.append(sh.shift(behinds[kind], got, kind, False))
        return aheads_out, behinds_out

    def smear_step(step, items):
        aheads, behinds = colour_hops(list(items), step)
        out = []
        for i, v in enumerate(items):
            total = None
            for part in aheads + behinds:
                total = part[i] if total is None else total + part[i]
            out.append((v + 0.25 * total) * 0.5)
        return tuple(out)

    def start_right(items):
        for i, v in enumerate(items):
            smt_out[0, i] = v
        smt_copy(0).start()
        for i, v in enumerate(flat(link_times(link, 3, unflat(items, 2), True))):
            smt_out[1, i] = v
        smt_copy(1).start()

    def finish_right(items):
        aheads, behinds = colour_hops(items, NSMEAR)
        smt_copy(0).wait_recv()
        got = unflat([smt_in[0, i] for i in range(12)], 2)
        aheads.append(flat(link_times(link, 3, got, False)))
        smt_copy(1).wait_recv()
        behinds.append([smt_in[1, i] for i in range(12)])
        diag = []
        for i, v in enumerate(items):
            total = None
            for part in aheads + behinds:
                total = part[i] if total is None else total + part[i]
            diag.append(v - HOP * total)
        diag = unflat(diag, 2)
        gs = [
            unflat([-HOP * (a - b) for a, b in zip(aheads[mu], behinds[mu])], 2)
            for mu in range(4)
        ]
        zero = jnp.zeros((8, 128), jnp.float32)

        def block(s2, s, q, a):
            if s2 == s:
                return diag[q][a]
            if s2 // 2 == s // 2:
                return (zero, zero)
            out = (zero, zero)
            for mu in range(4):
                for row in range(2):
                    column, coef = E_ROWS[mu][row]
                    if s2 < 2 and row == s2 and column == s - 2:
                        out = add_term(out, coef, gs[mu][q][a])
                    if s2 >= 2 and column == s2 - 2 and row == s:
                        out = add_term(out, complex(coef).conjugate(), gs[mu][q][a])
            return out

        for s2 in range(4):
            for a in range(3):
                column = [block(s2, s, 0, a) for s in range(4)]
                lone = [block(s2, s, 1, a) for s in range(4)]
                for part in range(2):
                    i = part * 12 + s2 * 3 + a
                    for s in range(4):
                        right[s, i] = column[s][part]
                    right[4, i] = jnp.where(sh.low, lone[0][part], lone[1][part])
                    right[5, i] = jnp.where(sh.low, lone[2][part], lone[3][part])

    def first_send(p, _):
        send_body(load_field(guess, p), 0, p, 1)
        return _

    row = lax.broadcasted_iota(jnp.int32, (8, 128), 0)
    hit = (row % 4 == sites_ref[1]) & (sh.lane == sites_ref[2] * LX + sites_ref[3])
    hit = hit & (sites_ref[0] == 0)
    one = jnp.where(hit, 1.0, 0.0).astype(jnp.float32)
    zero = jnp.zeros((8, 128), jnp.float32)
    upper, lower = jnp.where(sh.low, one, 0.0), jnp.where(sh.low, 0.0, one)
    items = tuple(flat([
        [(upper, zero), (lower, zero), (zero, zero)],
        [(zero, zero), (zero, zero), (one, zero)],
    ]))

    lax.fori_loop(0, PAIRS, first_send, 0)
    items = lax.fori_loop(0, NSMEAR // 2, smear_step, items)
    interior(guess, 1)

    def second(p, _):
        out = receive_body(guess, 0, p, 1)
        for i, v in enumerate(out):
            field_a[p, i] = v
        send_body(unflat(out, 4), 1, p, -1)
        return _

    lax.fori_loop(0, PAIRS, second, 0)
    items = lax.fori_loop(NSMEAR // 2, NSMEAR, smear_step, items)
    items = list(items)
    start_right(items)
    finish_right(items)
    interior(field_a, -1)

    def third(p, _):
        out = receive_body(field_a, 1, p, -1)
        out = [right[p, i] - v for i, v in enumerate(out)]
        total = None
        for i, v in enumerate(out):
            search[p, i] = v
            total = v * v if total is None else total + v * v
        sums[p] = total
        send_body(unflat(out, 4), 2, p, 1)
        return _

    lax.fori_loop(0, PAIRS, third, 0)
    interior(search, 1)

    def fourth(p, _):
        out = receive_body(search, 2, p, 1)
        total = None
        for i, v in enumerate(out):
            field_b[p, i] = v
            total = v * v if total is None else total + v * v
        sums[PAIRS + p] = total
        send_body(unflat(out, 4), 3, p, -1)
        return _

    lax.fori_loop(0, PAIRS, fourth, 0)

    mine = jnp.zeros((8, 128), jnp.float32)
    for k in range(2 * PAIRS):
        mine = jnp.where(sh.lane == k, jnp.sum(sums[k], axis=1, keepdims=True), mine)
    slot = 0
    done_interior = False
    for stage, axis in enumerate(AXES):
        red_out[stage] = mine
        copies = []
        for k in range(1, n_of[axis]):
            copy = pltpu.make_async_remote_copy(
                src_ref=red_out.at[stage], dst_ref=red_in.at[slot],
                send_sem=r_send.at[slot], recv_sem=red_sem.at[slot],
                device_id=peer(axis, k), device_id_type=MESH,
            )
            copy.start()
            copies.append((copy, slot))
            slot += 1
        if not done_interior:
            interior(field_b, -1)
            done_interior = True
        for copy, place in copies:
            copy.wait()
            mine = mine + red_in[place]
    top = jnp.sum(mine[0:4], axis=0, keepdims=True)
    bottom = jnp.sum(mine[4:8], axis=0, keepdims=True)
    both = jnp.where(sh.low, top, bottom)
    curvature = pltpu.roll(both, 128 - PAIRS, 1)
    steps = both / jnp.where(sh.lane < PAIRS, curvature, 1.0)

    def last(p, _):
        out = receive_body(field_b, 3, p, -1)
        length = jnp.sum(jnp.where(sh.lane == p, steps, 0.0), axis=1, keepdims=True)
        first, second_rhs = rhs_of(p)
        for i, v in enumerate(out):
            s = search[p, i]
            res = s - length * v
            sol = guess[p, i] + length * s
            res_ref[first, i] = res[0:4]
            res_ref[second_rhs, i] = res[4:8]
            sol_ref[first, i] = sol[0:4]
            sol_ref[second_rhs, i] = sol[4:8]
        return _

    lax.fori_loop(0, PAIRS, last, 0)

    def drain_w(p, _):
        for w in range(4):
            for d in range(4):
                edge_copy(w, d, p).wait_send()
            for d in range(2):
                time_copy(w, d, p).wait_send()
        return _

    lax.fori_loop(0, PAIRS, drain_w, 0)

    def drain_s(step, _):
        for d in range(4):
            sm_copy(step, d).wait_send()
        return _

    lax.fori_loop(0, NSMEAR + 1, drain_s, 0)
    for d in range(2):
        smt_copy(d).wait_send()


def on_device(sizes, links, guess, source_sites):
    rows, lanes = guess.shape[-2:]
    f32 = jnp.float32
    copies = sum(n - 1 for n in sizes)
    tile = (8, lanes)
    vm = lambda *shape: pltpu.VMEM(shape + tile, f32)
    dma = lambda *shape: pltpu.SemaphoreType.DMA(shape)
    out = jax.ShapeDtypeStruct((12, 24, rows, lanes), f32)
    sol, res = pl.pallas_call(
        functools.partial(kernel, sizes),
        out_shape=(out, out),
        in_specs=[
            pl.BlockSpec(memory_space=pltpu.SMEM),
            pl.BlockSpec(memory_space=pltpu.VMEM),
            pl.BlockSpec(memory_space=pltpu.VMEM),
        ],
        out_specs=(pl.BlockSpec(memory_space=pltpu.VMEM), pl.BlockSpec(memory_space=pltpu.VMEM)),
        scratch_shapes=[
            vm(72), vm(PAIRS, 24), vm(PAIRS, 24), vm(PAIRS, 24), vm(PAIRS, 24), vm(PAIRS, 24),
            vm(PAIRS, 24), vm(2, PAIRS, 12),
            vm(4, 4, PAIRS, 3), vm(4, 4, PAIRS, 3), vm(4, 2, PAIRS, 12), vm(4, 2, PAIRS, 12),
            vm(NSMEAR + 1, 4, 3), vm(NSMEAR + 1, 4, 3), vm(2, 12), vm(2, 12),
            vm(3), vm(copies), vm(2 * PAIRS),
            dma(4, 4, PAIRS), dma(4, 2, PAIRS), dma(4, 6, PAIRS),
            dma(NSMEAR + 1, 4), dma(2), dma(NSMEAR + 2, 4), dma(copies), dma(copies),
        ],
        compiler_params=pltpu.CompilerParams(
            collective_id=0, has_side_effects=True, vmem_limit_bytes=48 * 1024 * 1024
        ),
    )(
        source_sites.reshape(4),
        links.reshape(72, rows, lanes),
        guess.reshape(12, 24, rows, lanes),
    )
    return sol.reshape(guess.shape), res.reshape(guess.shape)


def solution(mesh):
    sizes = tuple(mesh.shape[axis] for axis in AXES)
    fields = P(None, None, None, None, "ta", "xy", "gz")
    return jax.shard_map(
        functools.partial(on_device, sizes),
        mesh=mesh,
        in_specs=(fields, fields, P("ta", "xy", "gz", None)),
        out_specs=(fields, fields),
        check_vma=False,
    )
```

profile of v0, /device:TPU:0, one launch (start us, length us, event | category | flops | bytes accessed | tf_op | source)
XLA Modules:
  0.0 80.3 jit_solution(12915164265432714276)
XLA Ops:
  0.6 0.0 copy-start.2
  0.6 0.6 copy-done.2
  1.3 0.0 copy-start
  1.3 1.1 %copy-done = f32[12,2,4,3,1,4,128]{6,5,4,3,2,1,0:T(4,128)S(1)} copy-done((f32[12,2,4,3,1,4,128]{6,5,4,3,2,1,0:T(4,128)S(1)}, f32[12,2,4,3,1,4,128]{6,5,4,3,2,1,0:T(4,128)}, u32[]{:S(2)}) %copy-start) | copy-done | bytes 589848
  2.4 0.0 copy-start.1
  2.4 0.9 %copy-done.1 = f32[4,2,3,3,1,4,128]{6,5,4,3,2,1,0:T(4,128)S(1)} copy-done((f32[4,2,3,3,1,4,128]{6,5,4,3,2,1,0:T(4,128)S(1)}, f32[4,2,3,3,1,4,128]{6,5,4,3,2,1,0:T(4,128)}, u32[]{:S(2)}) %copy-start.1) | copy-done | bytes 147480
  3.3 75.4 %shard_map.50 = (f32[12,24,4,128]{3,2,1,0:T(4,128)S(1)}, f32[12,24,4,128]{3,2,1,0:T(4,128)S(1)}) custom-call(s32[4]{0:T(128)S(1)} %bitcast.13, f32[72,4,128]{2,1,0:T(4,128)S(1)} %bitcast.12, f32[12,24,4,128]{3,2,1,0:T(4,128)S(1)} %bitcast.9), custom_call_target="tpu_custom_call" | custom-call | tf_op jit(solution)/shard_map/pallas_call | solution.py:493
  78.7 0.8 %copy.9 = f32[12,2,4,3,1,4,128]{6,5,4,3,2,1,0:T(4,128)} copy(f32[12,2,4,3,1,4,128]{6,5,4,3,2,1,0:T(4,128)S(1)} %bitcast.11) | data formatting | bytes 1179648
  79.5 0.8 %copy.10 = f32[12,2,4,3,1,4,128]{6,5,4,3,2,1,0:T(4,128)} copy(f32[12,2,4,3,1,4,128]{6,5,4,3,2,1,0:T(4,128)S(1)} %bitcast.10) | data formatting | bytes 1179648
Async XLA Ops:
  0.6 0.7 copy-start.2
  1.3 1.1 %copy-start = (f32[12,2,4,3,1,4,128]{6,5,4,3,2,1,0:T(4,128)S(1)}, f32[12,2,4,3,1,4,128]{6,5,4,3,2,1,0:T(4,128)}, u32[]{:S(2)}) copy-start(f32[12,2,4,3,1,4,128]{6,5,4,3,2,1,0:T(4,128)} %param.4) | copy-start | bytes 1769476
  2.4 0.9 %copy-start.1 = (f32[4,2,3,3,1,4,128]{6,5,4,3,2,1,0:T(4,128)S(1)}, f32[4,2,3,3,1,4,128]{6,5,4,3,2,1,0:T(4,128)}, u32[]{:S(2)}) copy-start(f32[4,2,3,3,1,4,128]{6,5,4,3,2,1,0:T(4,128)} %param.3) | copy-start | bytes 442372
where the time goes:
time: 80.5 us; the launch traced here: 80.3 us
  Pallas kernels  75.4 us (94%)
  local copies, waits for them, and re-layouts  4.25 us (5%)
    pallas_call x1, Pallas kernels, on_device(): pl.pallas_call(functools.partial(kernel, sizes), out_shape=(out, out), in...  75.4 us
    unnamed x8, local copies, waits for them, and re-layouts  4.25 us

commit v1 on v0

--- a/solution.py
+++ b/solution.py
@@ -11,6 +11,8 @@
 NSMEAR = 8
 HOP = 0.12
 PAIRS = 6
+EDGE_CHUNK = 3
+TIME_CHUNK = 1
 MESH = pl.DeviceIdType.MESH
 AXES = ("xy", "gz", "ta")
 
@@ -186,17 +188,37 @@
     lax.fori_loop(0, PAIRS, load_guess, 0)
     pl.semaphore_wait(barrier, sum(n - 1 for n in sizes))
 
+    def part_of(p, chunk):
+        return pl.ds(p, chunk)
+
+    def start_last(make, w, d, p, chunk):
+        if chunk == 1:
+            make(w, d, p).start()
+        else:
+            @pl.when(lax.rem(p, chunk) == chunk - 1)
+            def _():
+                make(w, d, p - (chunk - 1)).start()
+
+    def await_first(make, w, p, chunk, dirs):
+        def wait():
+            for d in dirs:
+                make(w, d, p).wait_recv()
+        if chunk == 1:
+            wait()
+        else:
+            pl.when(lax.rem(p, chunk) == 0)(wait)
+
     def edge_copy(w, d, p):
         axis, step = (("xy", -1), ("xy", 1), ("gz", -1), ("gz", 1))[d]
         return pltpu.make_async_remote_copy(
-            src_ref=edge_out.at[w, d, p], dst_ref=edge_in.at[w, d, p],
+            src_ref=edge_out.at[w, d, part_of(p, EDGE_CHUNK)], dst_ref=edge_in.at[w, d, part_of(p, EDGE_CHUNK)],
             send_sem=w_send.at[w, d, p], recv_sem=edge_sem.at[w, d, p],
             device_id=peer(axis, step), device_id_type=MESH,
         )
 
     def time_copy(w, d, p):
         return pltpu.make_async_remote_copy(
-            src_ref=time_out.at[w, d, p], dst_ref=time_in.at[w, d, p],
+            src_ref=time_out.at[w, d, part_of(p, TIME_CHUNK)], dst_ref=time_in.at[w, d, part_of(p, TIME_CHUNK)],
             send_sem=w_send.at[w, 4 + d, p], recv_sem=time_sem.at[w, d, p],
             device_id=peer("ta", (-1, 1)[d]), device_id_type=MESH,
         )
@@ -207,20 +229,20 @@
     def send_body(f, w, p, par):
         for i, v in enumerate(flat(project(f, 3, -par))):
             time_out[w, 0, p, i] = v
-        time_copy(w, 0, p).start()
+        start_last(time_copy, w, 0, p, TIME_CHUNK)
         for i, v in enumerate(flat(link_times(link, 3, project(f, 3, par), True))):
             time_out[w, 1, p, i] = v
-        time_copy(w, 1, p).start()
+        start_last(time_copy, w, 1, p, TIME_CHUNK)
         for kind, mu in ((0, 1), (1, 2)):
             for i, v in enumerate(sh.pack(flat(project(f, mu, -par)), kind, True)):
                 edge_out[w, 2 * kind, p, i] = v
-            edge_copy(w, 2 * kind, p).start()
+            start_last(edge_copy, w, 2 * kind, p, EDGE_CHUNK)
             behind = flat(link_times(link, mu, project(f, mu, par), True))
             for i, v in enumerate(behind):
                 carried[kind, p, i] = v
             for i, v in enumerate(sh.pack(behind, kind, False)):
                 edge_out[w, 2 * kind + 1, p, i] = v
-            edge_copy(w, 2 * kind + 1, p).start()
+            start_last(edge_copy, w, 2 * kind + 1, p, EDGE_CHUNK)
 
     def interior(src, par):
         def body(p, _):
@@ -237,21 +259,19 @@
         lax.fori_loop(0, PAIRS, body, 0)
 
     def receive_body(src, w, p, par):
+        await_first(edge_copy, w, p, EDGE_CHUNK, range(4))
+        await_first(time_copy, w, p, TIME_CHUNK, range(2))
         f = load_field(src, p)
         total = load_field(acc, p)
         for kind, mu in ((0, 1), (1, 2)):
-            edge_copy(w, 2 * kind, p).wait_recv()
             got = [edge_in[w, 2 * kind, p, i] for i in range(3)]
             ahead = unflat(sh.shift(flat(project(f, mu, -par)), got, kind, True), 2)
             lift_add(total, link_times(link, mu, ahead, False), mu, -par)
-            edge_copy(w, 2 * kind + 1, p).wait_recv()
             got = [edge_in[w, 2 * kind + 1, p, i] for i in range(3)]
             local = [carried[kind, p, i] for i in range(12)]
             lift_add(total, unflat(sh.shift(local, got, kind, False), 2), mu, par)
-        time_copy(w, 0, p).wait_recv()
         ahead = unflat([time_in[w, 0, p, i] for i in range(12)], 2)
         lift_add(total, link_times(link, 3, ahead, False), 3, -par)
-        time_copy(w, 1, p).wait_recv()
         lift_add(total, unflat([time_in[w, 1, p, i] for i in range(12)], 2), 3, par)
         return [a - HOP * b for a, b in zip(flat(f), flat(total))]
 
@@ -270,7 +290,7 @@
             device_id=peer("ta", (-1, 1)[d]), device_id_type=MESH,
         )
 
-    def colour_hops(items, step):
+    def colour_hops(items, step, beside):
         vectors = unflat(items, 2)
         behinds = []
         for kind, mu in ((0, 1), (1, 2)):
@@ -282,6 +302,11 @@
             for i, v in enumerate(sh.pack(behind, kind, False)):
                 sm_out[step, 2 * kind + 1, i] = v
             sm_copy(step, 2 * kind + 1).start()
+        for body, first, end in beside:
+            if body in (interior_guess, interior_field):
+                body()
+            else:
+                lax.fori_loop(first, end, body, 0)
         aheads_out = [flat(link_times(link, 0, unflat(sh.along_x(items, True), 2), False))]
         behinds_out = [sh.along_x(flat(link_times(link, 0, vectors, True)), False)]
         for kind, mu in ((0, 1), (1, 2)):
@@ -294,8 +319,8 @@
             behinds_out.append(sh.shift(behinds[kind], got, kind, False))
         return aheads_out, behinds_out
 
-    def smear_step(step, items):
-        aheads, behinds = colour_hops(list(items), step)
+    def smear_step(step, items, beside):
+        aheads, behinds = colour_hops(list(items), step, beside)
         out = []
         for i, v in enumerate(items):
             total = None
@@ -312,8 +337,8 @@
             smt_out[1, i] = v
         smt_copy(1).start()
 
-    def finish_right(items):
-        aheads, behinds = colour_hops(items, NSMEAR)
+    def finish_right(items, beside):
+        aheads, behinds = colour_hops(items, NSMEAR, beside)
         smt_copy(0).wait_recv()
         got = unflat([smt_in[0, i] for i in range(12)], 2)
         aheads.append(flat(link_times(link, 3, got, False)))
@@ -373,9 +398,11 @@
         [(zero, zero), (zero, zero), (one, zero)],
     ]))
 
-    lax.fori_loop(0, PAIRS, first_send, 0)
-    items = lax.fori_loop(0, NSMEAR // 2, smear_step, items)
-    interior(guess, 1)
+    def interior_guess():
+        interior(guess, 1)
+
+    def interior_field():
+        interior(field_a, -1)
 
     def second(p, _):
         out = receive_body(guess, 0, p, 1)
@@ -384,16 +411,13 @@
         send_body(unflat(out, 4), 1, p, -1)
         return _
 
-    lax.fori_loop(0, PAIRS, second, 0)
-    items = lax.fori_loop(NSMEAR // 2, NSMEAR, smear_step, items)
-    items = list(items)
-    start_right(items)
-    finish_right(items)
-    interior(field_a, -1)
+    def normal(p, _):
+        for i, v in enumerate(receive_body(field_a, 1, p, -1)):
+            search[p, i] = v
+        return _
 
     def third(p, _):
-        out = receive_body(field_a, 1, p, -1)
-        out = [right[p, i] - v for i, v in enumerate(out)]
+        out = [right[p, i] - search[p, i] for i in range(24)]
         total = None
         for i, v in enumerate(out):
             search[p, i] = v
@@ -401,6 +425,23 @@
         sums[p] = total
         send_body(unflat(out, 4), 2, p, 1)
         return _
+
+    beside = {
+        0: [(first_send, 0, 6)],
+        1: [(interior_guess, 0, 0)],
+        2: [(second, 0, 2)],
+        3: [(second, 2, 4)],
+        4: [(second, 4, 6)],
+        5: [(interior_field, 0, 0)],
+        6: [(normal, 0, 2)],
+        7: [(normal, 2, 4)],
+        8: [(normal, 4, 6)],
+    }
+    for step in range(NSMEAR):
+        items = smear_step(step, items, beside.get(step, []))
+    items = list(items)
+    start_right(items)
+    finish_right(items, beside[NSMEAR])
 
     lax.fori_loop(0, PAIRS, third, 0)
     interior(search, 1)
@@ -462,15 +503,16 @@
 
     lax.fori_loop(0, PAIRS, last, 0)
 
-    def drain_w(p, _):
-        for w in range(4):
+    def drain(w, _):
+        for p in range(0, PAIRS, EDGE_CHUNK):
             for d in range(4):
                 edge_copy(w, d, p).wait_send()
+        for p in range(0, PAIRS, TIME_CHUNK):
             for d in range(2):
                 time_copy(w, d, p).wait_send()
         return _
 
-    lax.fori_loop(0, PAIRS, drain_w, 0)
+    lax.fori_loop(0, 4, drain, 0)
 
     def drain_s(step, _):
         for d in range(4):

time: 80.5 us -> 73.3 us (0.911)
  Pallas kernels: 75.4 us -> 68.2 us
    pallas_call x1, Pallas kernels: 75.4 us -> 68.2 us  [on_device(): pl.pallas_call(functools.partial(kernel, sizes), out_shape=(out, out), in...]
where the time goes in v1:
time: 73.3 us; the launch traced here: 73.1 us
  Pallas kernels  68.2 us (93%)
  local copies, waits for them, and re-layouts  4.25 us (6%)
    pallas_call x1, Pallas kernels, on_device(): pl.pallas_call(functools.partial(kernel, sizes), out_shape=(out, out), in...  68.2 us
    unnamed x8, local copies, waits for them, and re-layouts  4.25 us

profile of v1, /device:TPU:0, one launch (start us, length us, event | category | flops | bytes accessed | tf_op | source)
XLA Modules:
  0.0 73.1 jit_solution(1320794182624914820)
XLA Ops:
  0.6 0.0 copy-start.2
  0.6 0.6 copy-done.2
  1.3 0.0 copy-start
  1.3 1.1 %copy-done = f32[12,2,4,3,1,4,128]{6,5,4,3,2,1,0:T(4,128)S(1)} copy-done((f32[12,2,4,3,1,4,128]{6,5,4,3,2,1,0:T(4,128)S(1)}, f32[12,2,4,3,1,4,128]{6,5,4,3,2,1,0:T(4,128)}, u32[]{:S(2)}) %copy-start) | copy-done | bytes 589848
  2.4 0.0 copy-start.1
  2.4 0.9 %copy-done.1 = f32[4,2,3,3,1,4,128]{6,5,4,3,2,1,0:T(4,128)S(1)} copy-done((f32[4,2,3,3,1,4,128]{6,5,4,3,2,1,0:T(4,128)S(1)}, f32[4,2,3,3,1,4,128]{6,5,4,3,2,1,0:T(4,128)}, u32[]{:S(2)}) %copy-start.1) | copy-done | bytes 147480
  3.3 68.2 %shard_map.50 = (f32[12,24,4,128]{3,2,1,0:T(4,128)S(1)}, f32[12,24,4,128]{3,2,1,0:T(4,128)S(1)}) custom-call(s32[4]{0:T(128)S(1)} %bitcast.13, f32[72,4,128]{2,1,0:T(4,128)S(1)} %bitcast.12, f32[12,24,4,128]{3,2,1,0:T(4,128)S(1)} %bitcast.9), custom_call_target="tpu_custom_call" | custom-call | tf_op jit(solution)/shard_map/pallas_call | solution.py:535
  71.5 0.8 %copy.9 = f32[12,2,4,3,1,4,128]{6,5,4,3,2,1,0:T(4,128)} copy(f32[12,2,4,3,1,4,128]{6,5,4,3,2,1,0:T(4,128)S(1)} %bitcast.11) | data formatting | bytes 1179648
  72.3 0.8 %copy.10 = f32[12,2,4,3,1,4,128]{6,5,4,3,2,1,0:T(4,128)} copy(f32[12,2,4,3,1,4,128]{6,5,4,3,2,1,0:T(4,128)S(1)} %bitcast.10) | data formatting | bytes 1179648
Async XLA Ops:
  0.6 0.7 copy-start.2
  1.3 1.1 %copy-start = (f32[12,2,4,3,1,4,128]{6,5,4,3,2,1,0:T(4,128)S(1)}, f32[12,2,4,3,1,4,128]{6,5,4,3,2,1,0:T(4,128)}, u32[]{:S(2)}) copy-start(f32[12,2,4,3,1,4,128]{6,5,4,3,2,1,0:T(4,128)} %param.4) | copy-start | bytes 1769476
  2.4 0.9 %copy-start.1 = (f32[4,2,3,3,1,4,128]{6,5,4,3,2,1,0:T(4,128)S(1)}, f32[4,2,3,3,1,4,128]{6,5,4,3,2,1,0:T(4,128)}, u32[]{:S(2)}) copy-start(f32[4,2,3,3,1,4,128]{6,5,4,3,2,1,0:T(4,128)} %param.3) | copy-start | bytes 442372

commit v2 on v1

--- a/solution.py
+++ b/solution.py
@@ -293,10 +293,11 @@
     def colour_hops(items, step, beside):
         vectors = unflat(items, 2)
         behinds = []
-        for kind, mu in ((0, 1), (1, 2)):
+        for kind in range(2):
             for i, v in enumerate(sh.pack(items, kind, True)):
                 sm_out[step, 2 * kind, i] = v
             sm_copy(step, 2 * kind).start()
+        for kind, mu in ((0, 1), (1, 2)):
             behind = flat(link_times(link, mu, vectors, True))
             behinds.append(behind)
             for i, v in enumerate(sh.pack(behind, kind, False)):

time: 73.3 us -> 73.4 us (level)
  no operation moved by 1% of the time
where the time goes in v2:
time: 73.4 us; the launch traced here: 73.2 us
  Pallas kernels  68.3 us (93%)
  local copies, waits for them, and re-layouts  4.25 us (6%)
    pallas_call x1, Pallas kernels, on_device(): pl.pallas_call(functools.partial(kernel, sizes), out_shape=(out, out), in...  68.3 us
    unnamed x8, local copies, waits for them, and re-layouts  4.25 us

profile of v2, /device:TPU:0, one launch (start us, length us, event | category | flops | bytes accessed | tf_op | source)
XLA Modules:
  0.0 73.2 jit_solution(5579695301641267340)
XLA Ops:
  0.6 0.0 copy-start.2
  0.6 0.6 copy-done.2
  1.3 0.0 copy-start
  1.3 1.1 %copy-done = f32[12,2,4,3,1,4,128]{6,5,4,3,2,1,0:T(4,128)S(1)} copy-done((f32[12,2,4,3,1,4,128]{6,5,4,3,2,1,0:T(4,128)S(1)}, f32[12,2,4,3,1,4,128]{6,5,4,3,2,1,0:T(4,128)}, u32[]{:S(2)}) %copy-start) | copy-done | bytes 589848
  2.4 0.0 copy-start.1
  2.4 0.9 %copy-done.1 = f32[4,2,3,3,1,4,128]{6,5,4,3,2,1,0:T(4,128)S(1)} copy-done((f32[4,2,3,3,1,4,128]{6,5,4,3,2,1,0:T(4,128)S(1)}, f32[4,2,3,3,1,4,128]{6,5,4,3,2,1,0:T(4,128)}, u32[]{:S(2)}) %copy-start.1) | copy-done | bytes 147480
  3.3 68.3 %shard_map.50 = (f32[12,24,4,128]{3,2,1,0:T(4,128)S(1)}, f32[12,24,4,128]{3,2,1,0:T(4,128)S(1)}) custom-call(s32[4]{0:T(128)S(1)} %bitcast.13, f32[72,4,128]{2,1,0:T(4,128)S(1)} %bitcast.12, f32[12,24,4,128]{3,2,1,0:T(4,128)S(1)} %bitcast.9), custom_call_target="tpu_custom_call" | custom-call | tf_op jit(solution)/shard_map/pallas_call | solution.py:536
  71.5 0.8 %copy.9 = f32[12,2,4,3,1,4,128]{6,5,4,3,2,1,0:T(4,128)} copy(f32[12,2,4,3,1,4,128]{6,5,4,3,2,1,0:T(4,128)S(1)} %bitcast.11) | data formatting | bytes 1179648
  72.4 0.8 %copy.10 = f32[12,2,4,3,1,4,128]{6,5,4,3,2,1,0:T(4,128)} copy(f32[12,2,4,3,1,4,128]{6,5,4,3,2,1,0:T(4,128)S(1)} %bitcast.10) | data formatting | bytes 1179648
Async XLA Ops:
  0.6 0.7 copy-start.2
  1.3 1.1 %copy-start = (f32[12,2,4,3,1,4,128]{6,5,4,3,2,1,0:T(4,128)S(1)}, f32[12,2,4,3,1,4,128]{6,5,4,3,2,1,0:T(4,128)}, u32[]{:S(2)}) copy-start(f32[12,2,4,3,1,4,128]{6,5,4,3,2,1,0:T(4,128)} %param.4) | copy-start | bytes 1769476
  2.4 0.9 %copy-start.1 = (f32[4,2,3,3,1,4,128]{6,5,4,3,2,1,0:T(4,128)S(1)}, f32[4,2,3,3,1,4,128]{6,5,4,3,2,1,0:T(4,128)}, u32[]{:S(2)}) copy-start(f32[4,2,3,3,1,4,128]{6,5,4,3,2,1,0:T(4,128)} %param.3) | copy-start | bytes 442372
